TPU v7x, 32 devices: a whole 2x2x4 slice. The times are simulated.
32 devices in a mesh: groups: 2 (over x), lon: 8 (over z, y), lat: 2 (over core).
Axes of the slice: x: 2, y: 2, z: 4, core: 2. Of those that a mesh axis runs over, the one named last changes fastest.
Arguments:
- fields: bfloat16 [24, 1024, 128], P(('groups', 'lat'), 'lon'), parts along dimension 0, may hold values from -6 to 6
- norm_gain: float32 [128], replicated, may hold values from 0.5 to 1.5
- w_qkv: bfloat16 [128, 384], replicated, may hold values from -5.303301 to 5.303301
- w_out: bfloat16 [128, 128], replicated, may hold values from -0.5 to 0.5
Outputs:
- updated: bfloat16 [24, 1024, 128], P(('groups', 'lat'), 'lon'), parts along dimension 0
There are 2 independent parts, one for each index of `groups`. A program takes and returns all parts, laid end to end along the dimension named above; an argument that names none is the same for every part. Nothing has to cross between parts.
All inputs are finite; a program needn't handle non-finite values.
Results may differ from a plain program's by a relative error of at most 0.005.
The roundings to bfloat16 on the way count: a program that leaves them out, or rounds other values in their place, can miss the bound.
Values may be sent and summed in bfloat16 or wider, within the bound.
A program may use at most 128 MiB of HBM per device.

v0:
```python
import functools
import math

import jax
import jax.numpy as jnp
from jax import lax
from jax.experimental import pallas as pl
from jax.experimental.pallas import tpu as pltpu
from jax.sharding import PartitionSpec as P

HEADS = 8
LOG2E = math.log2(math.e)
MESH = pl.DeviceIdType.MESH


def dot(a, b, contract):
    return lax.dot_general(a, b, ((contract[:1], contract[1:]), ((), ())), preferred_element_type=jnp.float32)


def kernel(n, per, slots, fields_ref, gain_ref, wqkv_ref, wout_ref, out_ref,
           normed, whole, w_t, scores_a, scores_b, scores_c, q_s, k_s, v_s,
           mixed, returned,
           send1, recv1, send2, recv2):
    me = lax.axis_index("lon")
    rows, cells, width = fields_ref.shape
    head_width = width // HEADS
    total = n * cells
    block = math.gcd(total, 512)
    chunk = math.gcd(total, 256)

    def partner(k):
        if n & (n - 1):
            return lax.rem(me + n - k, n)
        mate = 0
        for bit in range(n.bit_length() - 1):
            own = lax.rem(me // (1 << bit), 2)
            mate = mate + ((1 - own) if (k >> bit) & 1 else own) * (1 << bit)
        return mate

    barrier = pltpu.get_barrier_semaphore()
    for k in range(1, n):
        pl.semaphore_signal(barrier, inc=1, device_id={"lon": lax.rem(me + k, n)}, device_id_type=MESH)

    gain = gain_ref[...]
    for r in range(rows):
        inputs = fields_ref[r].astype(jnp.float32)
        center = jnp.mean(inputs, axis=-1, keepdims=True)
        spread = jnp.mean((inputs - center) ** 2, axis=-1, keepdims=True)
        normed[r] = ((inputs - center) * lax.rsqrt(spread + 1e-05) * gain).astype(jnp.bfloat16)

    def first_row(d):
        return (d * per) // HEADS

    def last_row(d):
        return (d * per + per - 1) // HEADS

    pl.semaphore_wait(barrier, n - 1)

    def forward(j, k):
        d = partner(k)
        return d, pltpu.make_async_remote_copy(
            src_ref=normed.at[first_row(d) + j],
            dst_ref=whole.at[j, me],
            send_sem=send1.at[j, k],
            recv_sem=recv1.at[j, me],
            device_id={"lon": d},
            device_id_type=MESH,
        )

    for j in range(slots):
        for k in range(n - 1, 0, -1):
            d, copy = forward(j, k)

            @pl.when(first_row(d) + j <= last_row(d))
            def _():
                copy.start()

    for j in range(slots):
        @pl.when(first_row(me) + j <= last_row(me))
        def _():
            whole[j, me] = normed[first_row(me) + j]

    w_t[...] = wqkv_ref[...].astype(jnp.float32).T.astype(jnp.bfloat16)

    def back(t, k):
        d = partner(k)
        return pltpu.make_async_remote_copy(
            src_ref=mixed.at[t, d],
            dst_ref=returned.at[me * per + t],
            send_sem=send2.at[t, k],
            recv_sem=recv2.at[me * per + t],
            device_id={"lon": d},
            device_id_type=MESH,
        )

    def wait_slot(slot):
        for k in range(1, n):
            src = lax.rem(me + k, n)
            pltpu.make_async_remote_copy(
                src_ref=normed.at[0],
                dst_ref=whole.at[slot, src],
                send_sem=send1.at[0, 0],
                recv_sem=recv1.at[slot, src],
                device_id={"lon": src},
                device_id_type=MESH,
            ).wait_recv()

    def project(item):
        head = lax.rem(item, HEADS)
        cell_rows = whole[item // HEADS - first_row(me)].reshape(total, width)

        def weight(part):
            start = pl.multiple_of(part * width + head * head_width, head_width)
            return w_t[pl.ds(start, head_width), :]

        w_k = weight(1)
        q_t = (dot(weight(0), cell_rows, (1, 1)) * (1.0 / math.sqrt(head_width))).astype(jnp.bfloat16)
        q_t = q_t.astype(jnp.float32) * LOG2E
        q_hi = q_t.astype(jnp.bfloat16)
        q_lo = (q_t - q_hi.astype(jnp.float32)).astype(jnp.bfloat16)
        q_s[...] = jnp.concatenate([q_hi, q_lo], axis=0)
        k_s[...] = dot(cell_rows, jnp.concatenate([w_k, w_k], axis=0), (1, 1)).astype(jnp.bfloat16)
        v_s[...] = dot(weight(2), cell_rows, (1, 1)).astype(jnp.bfloat16)

    def buffer(b):
        return scores_c if b == 0 else (scores_a, scores_b)[b % 2]

    def first_pass(b, queries, keys):
        q_block = queries[:, b * block:(b + 1) * block]
        highest = None
        for c in range(total // chunk):
            s = dot(keys[c * chunk:(c + 1) * chunk], q_block, (1, 0))
            buffer(b)[pl.ds(c * chunk, chunk), :] = s
            part = jnp.max(s.reshape(chunk // 8, 8, block), axis=0)
            highest = part if highest is None else jnp.maximum(highest, part)
        return jnp.max(highest, axis=0, keepdims=True)

    def second_pass(b, highest, v_t):
        sums = jnp.zeros((8, block), jnp.float32)
        acc = jnp.zeros((head_width, block), jnp.float32)
        for c in range(total // chunk):
            p = jnp.exp2(buffer(b)[pl.ds(c * chunk, chunk), :] - highest)
            sums = sums + jnp.sum(p.reshape(chunk // 8, 8, block), axis=0)
            acc = acc + dot(v_t[:, c * chunk:(c + 1) * chunk], p.astype(jnp.bfloat16), (1, 0))
        return (acc / jnp.sum(sums, axis=0, keepdims=True)).astype(jnp.bfloat16)

    def one_item(t, highest):
        item = me * per + t
        after = jnp.minimum(item + 1, me * per + per - 1)

        @pl.when((t + 1 < per) & (lax.rem(item + 1, HEADS) == 0))
        def _():
            wait_slot(after // HEADS - first_row(me))

        queries, keys, v_t = q_s[...], k_s[...], v_s[...]
        project(after)
        blocks = total // block
        for b in range(blocks):
            if b + 1 < blocks:
                following = first_pass(b + 1, queries, keys)
            done = second_pass(b, highest, v_t)
            if b + 1 == blocks:
                following = first_pass(0, q_s[...], k_s[...])
            highest = following
            for s in range(block // cells):
                mixed[t, b * (block // cells) + s] = done[:, s * cells:(s + 1) * cells]

        returned[item] = mixed[t, me]
        for k in range(n - 1, 0, -1):
            back(t, k).start()
        return highest

    wait_slot(0)
    project(me * per)
    lax.fori_loop(0, per, one_item, first_pass(0, q_s[...], k_s[...]))

    def finish(t, carry):
        for k in range(1, n):
            src = lax.rem(me + k, n)
            pltpu.make_async_remote_copy(
                src_ref=mixed.at[0, 0],
                dst_ref=returned.at[src * per + t],
                send_sem=send2.at[t, k],
                recv_sem=recv2.at[src * per + t],
                device_id={"lon": src},
                device_id_type=MESH,
            ).wait_recv()
        return carry

    lax.fori_loop(0, per, finish, 0)

    for r in range(rows):
        att_t = returned[pl.ds(r * HEADS, HEADS)].reshape(width, cells)
        update = dot(att_t, wout_ref[...], (0, 0))
        out_ref[r] = (fields_ref[r].astype(jnp.float32) + update).astype(jnp.bfloat16)

    for j in range(slots):
        for k in range(1, n):
            d, copy = forward(j, k)

            @pl.when(first_row(d) + j <= last_row(d))
            def _():
                copy.wait_send()

    def sent(t, carry):
        for k in range(1, n):
            back(t, k).wait_send()
        return carry

    lax.fori_loop(0, per, sent, 0)


def solution(mesh):
    n = mesh.shape["lon"]

    def body(fields, norm_gain, w_qkv, w_out):
        rows, cells, width = fields.shape
        per = rows * HEADS // n
        slots = max((d * per + per - 1) // HEADS - (d * per) // HEADS + 1 for d in range(n))
        total = n * cells
        block = math.gcd(total, 512)
        return pl.pallas_call(
            functools.partial(kernel, n, per, slots),
            out_shape=jax.ShapeDtypeStruct(fields.shape, fields.dtype),
            in_specs=[pl.BlockSpec(memory_space=pltpu.VMEM)] * 4,
            out_specs=pl.BlockSpec(memory_space=pltpu.VMEM),
            scratch_shapes=[
                pltpu.VMEM((rows, cells, width), jnp.bfloat16),
                pltpu.VMEM((slots, n, cells, width), jnp.bfloat16),
                pltpu.VMEM((3 * width, width), jnp.bfloat16),
                pltpu.VMEM((total, block), jnp.float32),
                pltpu.VMEM((total, block), jnp.float32),
                pltpu.VMEM((total, block), jnp.float32),
                pltpu.VMEM((2 * width // HEADS, total), jnp.bfloat16),
                pltpu.VMEM((total, 2 * width // HEADS), jnp.bfloat16),
                pltpu.VMEM((width // HEADS, total), jnp.bfloat16),
                pltpu.VMEM((per, n, width // HEADS, cells), jnp.bfloat16),
                pltpu.VMEM((rows * HEADS, width // HEADS, cells), jnp.bfloat16),
                pltpu.SemaphoreType.DMA((slots, n)),
                pltpu.SemaphoreType.DMA((slots, n)),
                pltpu.SemaphoreType.DMA((per, n)),
                pltpu.SemaphoreType.DMA((rows * HEADS,)),
            ],
            compiler_params=pltpu.CompilerParams(collective_id=0, has_side_effects=True),
        )(fields, norm_gain.reshape(1, width), w_qkv, w_out)

    return jax.shard_map(
        body,
        mesh=mesh,
        in_specs=(P(("groups", "lat"), "lon", None), P(), P(), P()),
        out_specs=P(("groups", "lat"), "lon", None),
        check_vma=False,
    )
```

profile of v0, /device:TPU:0, one launch (start us, length us, event | category | flops | bytes accessed | tf_op | source)
XLA Modules:
  0.0 33.6 jit_solution(7000151558387644698)
XLA Ops:
  0.0 31.9 %shard_map.46 = bf16[6,128,128]{2,1,0:T(8,128)(2,1)} custom-call(bf16[6,128,128]{2,1,0:T(8,128)(2,1)} %fields_ref.1, f32[1,128]{1,0:T(1,128)} %bitcast.1, bf16[128,384]{1,0:T(8,128)(2,1)} %wqkv_ref.1, bf16[128,128]{1,0:T(8,128)(2,1)} %wout_ref.1), custom_call_target="tpu_custom_call" | custom-call | tf_op jit(solution)/shard_map/pallas_call | solution.py:222
  32.0 1.6 %copy.6 = bf16[6,128,128]{2,1,0:T(8,128)(2,1)} copy(bf16[6,128,128]{2,1,0:T(8,128)(2,1)} %shard_map.46) | data formatting | bytes 393216
where the time goes:
time: 33.7 us; the launch traced here: 33.6 us
  Pallas kernels  31.9 us (95%)
  local copies, waits for them, and re-layouts  1.62 us (5%)
    pallas_call x1, Pallas kernels, body(): pl.pallas_call(functools.partial(kernel, n, per, slots), out_shape=jax.Sh...  31.9 us
    unnamed x1, local copies, waits for them, and re-layouts  1.62 us

commit v1 on v0

--- a/solution.py
+++ b/solution.py
@@ -17,7 +17,8 @@
     return lax.dot_general(a, b, ((contract[:1], contract[1:]), ((), ())), preferred_element_type=jnp.float32)
 
 
-def kernel(n, per, slots, fields_ref, gain_ref, wqkv_ref, wout_ref, out_ref,
+def kernel(n, per, slots, fields_hbm, gain_hbm, wqkv_hbm, wout_hbm, out_ref,
+           fields_ref, gain_ref, wqkv_ref, wout_ref, loaded,
            normed, whole, w_t, scores_a, scores_b, scores_c, q_s, k_s, v_s,
            mixed, returned,
            send1, recv1, send2, recv2):
@@ -40,6 +41,17 @@
     barrier = pltpu.get_barrier_semaphore()
     for k in range(1, n):
         pl.semaphore_signal(barrier, inc=1, device_id={"lon": lax.rem(me + k, n)}, device_id_type=MESH)
+
+    loads = [
+        pltpu.make_async_copy(src, dst, loaded.at[i])
+        for i, (src, dst) in enumerate((
+            (fields_hbm, fields_ref), (gain_hbm, gain_ref), (wqkv_hbm, wqkv_ref), (wout_hbm, wout_ref),
+        ))
+    ]
+    for load in loads:
+        load.start()
+    for load in loads:
+        load.wait()
 
     gain = gain_ref[...]
     for r in range(rows):
@@ -221,10 +233,15 @@
         block = math.gcd(total, 512)
         return pl.pallas_call(
             functools.partial(kernel, n, per, slots),
-            out_shape=jax.ShapeDtypeStruct(fields.shape, fields.dtype),
-            in_specs=[pl.BlockSpec(memory_space=pltpu.VMEM)] * 4,
+            out_shape=pltpu.VMEM(fields.shape, fields.dtype),
+            in_specs=[pl.BlockSpec(memory_space=pltpu.HBM)] * 4,
             out_specs=pl.BlockSpec(memory_space=pltpu.VMEM),
             scratch_shapes=[
+                pltpu.VMEM(fields.shape, fields.dtype),
+                pltpu.VMEM((1, width), norm_gain.dtype),
+                pltpu.VMEM(w_qkv.shape, w_qkv.dtype),
+                pltpu.VMEM(w_out.shape, w_out.dtype),
+                pltpu.SemaphoreType.DMA((4,)),
                 pltpu.VMEM((rows, cells, width), jnp.bfloat16),
                 pltpu.VMEM((slots, n, cells, width), jnp.bfloat16),
                 pltpu.VMEM((3 * width, width), jnp.bfloat16),
@@ -241,8 +258,13 @@
                 pltpu.SemaphoreType.DMA((per, n)),
                 pltpu.SemaphoreType.DMA((rows * HEADS,)),
             ],
-            compiler_params=pltpu.CompilerParams(collective_id=0, has_side_effects=True),
-        )(fields, norm_gain.reshape(1, width), w_qkv, w_out)
+            compiler_params=pltpu.CompilerParams(
+                collective_id=0, has_side_effects=True, vmem_limit_bytes=40 * 2**20,
+            ),
+        )(*(
+            pltpu.with_memory_space_constraint(x, pltpu.HBM)
+            for x in (fields, norm_gain.reshape(1, width), w_qkv, w_out)
+        ))
 
     return jax.shard_map(
         body,

time: 33.7 us -> 31.1 us (0.923)
  Pallas kernels: 31.9 us -> 30.3 us
  local copies, waits for them, and re-layouts: 1.62 us -> 0.68 us
    pallas_call x1, Pallas kernels: 31.9 us -> 30.3 us  [body(): pl.pallas_call(functools.partial(kernel, n, per, slots), out_shape=pltpu....]
    unnamed x1, local copies, waits for them, and re-layouts: 1.62 us -> 0.68 us
where the time goes in v1:
time: 31.1 us; the launch traced here: 31 us
  Pallas kernels  30.3 us (97%)
  local copies, waits for them, and re-layouts  0.68 us (2%)
    pallas_call x1, Pallas kernels, body(): pl.pallas_call(functools.partial(kernel, n, per, slots), out_shape=pltpu....  30.3 us
    unnamed x1, local copies, waits for them, and re-layouts  0.68 us

profile of v1, /device:TPU:0, one launch (start us, length us, event | category | flops | bytes accessed | tf_op | source)
XLA Modules:
  0.0 31.0 jit_solution(9323407488981794547)
XLA Ops:
  0.0 30.3 %shard_map.46 = bf16[6,128,128]{2,1,0:T(8,128)(2,1)S(1)} custom-call(bf16[6,128,128]{2,1,0:T(8,128)(2,1)} %fields_hbm.1, f32[1,128]{1,0:T(1,128)} %bitcast.1, bf16[128,384]{1,0:T(8,128)(2,1)} %wqkv_hbm.1, bf16[128,128]{1,0:T(8,128)(2,1)} %wout_hbm.1), custom_call_target="tpu_custom_call" | custom-call | tf_op jit(solution)/shard_map/pallas_call | solution.py:234
  30.3 0.7 %copy.6 = bf16[6,128,128]{2,1,0:T(8,128)(2,1)} copy(bf16[6,128,128]{2,1,0:T(8,128)(2,1)S(1)} %shard_map.46) | data formatting | bytes 393216

commit v2 on v1

v2 whole, which is shorter than its diff:
```python
import functools
import math

import jax
import jax.numpy as jnp
from jax import lax
from jax.experimental import pallas as pl
from jax.experimental.pallas import tpu as pltpu
from jax.sharding import PartitionSpec as P

HEADS = 8
LOG2E = math.log2(math.e)
MESH = pl.DeviceIdType.MESH


def dot(a, b, contract):
    return lax.dot_general(a, b, ((contract[:1], contract[1:]), ((), ())), preferred_element_type=jnp.float32)


def plan(n, m, rows):
    chips = max(c for c in range(m, n // 2 + 1, m) if n % c == 0 and (rows * m) % c == 0)
    rpc = rows * m // chips
    return chips, rpc, rpc // m


def kernel(n, m, fields_hbm, gain_hbm, wqkv_hbm, wout_hbm, out_ref,
           fields_ref, gain_ref, wqkv_ref, wout_ref,
           normed, w_t, x, scores_a, scores_b, q_s, kk_s, v_s, top_s, sum_s, acc_s, mixed, returned,
           loaded, send1, twin1, recv1, relayed, send2, recv2):
    me, lat = lax.axis_index("lon"), lax.axis_index("lat")
    rows, cells, width = fields_ref.shape
    head_width = width // HEADS
    chips, rpc, full = plan(n, m, rows)
    groups = n // chips
    share = HEADS // m
    half = share * head_width
    queries = chips * cells
    pair = 2
    block = pair * cells
    blocks = chips // pair
    per_lat = chips // m
    group, chip = me // chips, lax.rem(me, chips)
    source_lat = chip // per_lat
    first_row = lax.rem(chip, per_lat) * rpc
    mine = source_lat == lat
    other = 1 - lat
    shared = full if rpc % m else None
    slots = list(range(full)) + ([full] if rpc % m else [])

    barrier = pltpu.get_barrier_semaphore()
    for k in range(n):
        for c in range(m):
            if k or c:
                pl.semaphore_signal(
                    barrier, inc=1, device_id={"lon": lax.rem(me + k, n), "lat": lax.rem(lat + c, m)},
                    device_id_type=MESH)

    loads = [
        pltpu.make_async_copy(src, dst, loaded.at[i])
        for i, (src, dst) in enumerate((
            (fields_hbm, fields_ref), (gain_hbm, gain_ref), (wqkv_hbm, wqkv_ref), (wout_hbm, wout_ref),
        ))
    ]
    for load in loads:
        load.start()
    loads[1].wait()
    loads[0].wait()

    gain = gain_ref[...]
    for r in range(rows):
        inputs = fields_ref[r].astype(jnp.float32)
        center = jnp.mean(inputs, axis=-1, keepdims=True)
        spread = jnp.mean((inputs - center) ** 2, axis=-1, keepdims=True)
        normed[r] = ((inputs - center) * lax.rsqrt(spread + 1e-05) * gain).astype(jnp.bfloat16)

    def slot_row(slot):
        if slot == shared:
            return first_row + full
        return first_row + slot + lat * (rpc - full)

    def remote(src, dst, send, recv, lon, core):
        return pltpu.make_async_remote_copy(
            src_ref=src, dst_ref=dst, send_sem=send, recv_sem=recv,
            device_id={"lon": lon, "lat": core}, device_id_type=MESH)

    def forward(k, r):
        lon = lax.rem(group + k, groups) * chips + lat * per_lat + r // rpc
        w = r % rpc
        if w < full:
            slot, core = w, 0
        elif w >= rpc - full:
            slot, core = w - (rpc - full), 1
        else:
            slot, core = full, lax.rem(me, m)
        away = True if k else (lon != me)
        if not k and slot != shared:
            away = (lon != me) | (core != lat)
        copy = remote(normed.at[r], x.at[slot, me], send1.at[k, r], recv1.at[slot, me], lon, core)
        twin = None
        if not k and slot == shared:
            twin = remote(normed.at[r], x.at[slot, me], twin1.at[r], recv1.at[slot, me], me, other)
        return slot, away, copy, twin

    order = [r for r in range(rows) if full <= r % rpc < rpc - full] + [
        r for r in range(rows) if not full <= r % rpc < rpc - full]

    def each_forward(use):
        for k in range(groups):
            for r in order:
                slot, away, copy, twin = forward(k, r)
                if away is True:
                    use(copy)
                    continue

                @pl.when(away)
                def _():
                    use(copy)

                if twin is not None:
                    @pl.when(jnp.logical_not(away))
                    def _():
                        use(twin)

    pl.semaphore_wait(barrier, n * m - 1)
    each_forward(lambda copy: copy.start())

    @pl.when(mine)
    def _():
        for slot in slots:
            x[slot, me] = normed[slot_row(slot)]

    loads[2].wait()
    loads[3].wait()
    w_t[...] = wqkv_ref[...].astype(jnp.float32).T.astype(jnp.bfloat16)
    top_s[...] = jnp.full(top_s.shape, -jnp.inf, jnp.float32)
    sum_s[...] = jnp.zeros(sum_s.shape, jnp.float32)
    acc_s[...] = jnp.zeros(acc_s.shape, jnp.float32)

    def arrival(slot, s):
        return remote(normed.at[0], x.at[slot, s], send1.at[0, 0], recv1.at[slot, s], s, lat)

    def relay(s):
        return remote(x.at[full, s], x.at[full, s], relayed.at[s], recv1.at[full, s], me, other)

    def pass_on(k):
        if shared is None:
            return
        for c in range(chips):
            s = lax.rem(group + k, groups) * chips + c

            @pl.when((s != me) & (lax.rem(s, m) == lat))
            def _():
                arrival(full, s).wait_recv()
                relay(s).start()

    def weight(part, slot):
        start = part * width
        if slot != shared:
            return w_t[start:start + width, :]
        return w_t[pl.ds(pl.multiple_of(start + lat * half, half), half), :]

    def await_source(slot, s):
        if slot == shared:
            due = jnp.where(s == me, jnp.logical_not(mine), lax.rem(s, m) != lat)
        else:
            due = (s != me) | jnp.logical_not(mine)

        @pl.when(due)
        def _():
            arrival(slot, s).wait_recv()

    def heads_of(slot):
        return share if slot == shared else HEADS

    def project_queries(slot):
        span = heads_of(slot) * head_width
        for b in range(blocks):
            cell_rows = x[slot, pl.ds(group * chips + b * pair, pair)].reshape(block, width)
            q_t = (dot(weight(0, slot), cell_rows, (1, 1)) * (1.0 / math.sqrt(head_width))).astype(jnp.bfloat16)
            q_t = q_t.astype(jnp.float32) * LOG2E
            q_hi = q_t.astype(jnp.bfloat16)
            q_lo = (q_t - q_hi.astype(jnp.float32)).astype(jnp.bfloat16)
            q_s[slot, 0:span, b * block:(b + 1) * block] = q_hi
            q_s[slot, width:width + span, b * block:(b + 1) * block] = q_lo

    def attend(slot, s0):
        heads = heads_of(slot)
        span = heads * head_width
        cell_rows = x[slot, pl.ds(s0, pair)].reshape(block, width)
        w_k = weight(1, slot)
        if slot == shared:
            kk_s[:, 0:2 * span] = dot(cell_rows, jnp.concatenate([w_k, w_k], axis=0), (1, 1)).astype(jnp.bfloat16)
        else:
            keys = dot(cell_rows, w_k, (1, 1)).astype(jnp.bfloat16)
            kk_s[:, 0:span] = keys
            kk_s[:, span:2 * span] = keys
        v_s[0:span, :] = dot(weight(2, slot), cell_rows, (1, 1)).astype(jnp.bfloat16)

        def gap(size):
            return [jnp.zeros((size, queries), jnp.bfloat16)] if size else []

        def first_pass(h):
            lo, hi = h * head_width, (h + 1) * head_width
            spread_q = jnp.concatenate(
                gap(lo) + [q_s[slot, lo:hi, :]] + gap(span - hi + lo) + [q_s[slot, width + lo:width + hi, :]]
                + gap(span - hi), axis=0)
            s = dot(kk_s[:, 0:2 * span], spread_q, (1, 0))
            (scores_a, scores_b)[h % 2][...] = s
            return jnp.max(jnp.max(s.reshape(block // 8, 8, queries), axis=0), axis=0, keepdims=True)

        def second_pass(h, highest):
            at = slot * HEADS + h
            before = top_s[at]
            now = jnp.maximum(before, highest)
            fade = jnp.exp2(before - now)
            top_s[at] = now
            p = jnp.exp2((scores_a, scores_b)[h % 2][...] - now)
            sum_s[at] = sum_s[at] * fade + jnp.sum(p.reshape(block // 8, 8, queries), axis=0)
            acc_s[at] = acc_s[at] * fade + dot(
                v_s[h * head_width:(h + 1) * head_width, :], p.astype(jnp.bfloat16), (1, 0))

        highest = first_pass(0)
        for h in range(heads):
            following = first_pass(h + 1) if h + 1 < heads else None
            second_pass(h, highest)
            highest = following

    def attend_group(slot, k):
        theirs = lax.rem(group + k, groups)

        def one_block(b, carry):
            at = jnp.where(theirs > group, b, blocks - 1 - b) if k else b
            s0 = theirs * chips + at * pair
            if k:
                for i in range(pair):
                    await_source(slot, s0 + i)
            attend(slot, s0)
            return carry

        if not k:
            for c in range(chips):
                await_source(slot, theirs * chips + c)
            project_queries(slot)
        lax.fori_loop(0, blocks, one_block, 0)

    def units(slot):
        return [0] if slot == shared else list(range(m))

    def back(slot, u, c):
        hf = lat if slot == shared else u
        row = slot_row(slot)
        lon = group * chips + c
        copy = remote(mixed.at[slot, u, c], returned.at[row, hf], send2.at[slot, u, c], recv2.at[row, hf],
                      lon, source_lat)
        return row, hf, (lon != me) | (source_lat != lat), copy

    def hand_back(slot):
        for u in units(slot):
            for j in range(share):
                at = slot * HEADS + u * share + j
                done = (acc_s[at] / jnp.sum(sum_s[at], axis=0, keepdims=True)).astype(jnp.bfloat16)
                for c in range(chips):
                    mixed[slot, u, c, j * head_width:(j + 1) * head_width, :] = done[:, c * cells:(c + 1) * cells]
            for c in range(chips):
                row, hf, away, copy = back(slot, u, c)

                @pl.when(away)
                def _():
                    copy.start()

                @pl.when(jnp.logical_not(away))
                def _():
                    returned[row, hf] = mixed[slot, u, c]

    for k in range(groups):
        pass_on(k)
        for slot in (slots if not k else slots[::-1]):
            attend_group(slot, k)
            if k == groups - 1:
                hand_back(slot)

    for r in range(rows):
        w = r % rpc
        lon = group * chips + lat * per_lat + r // rpc
        for hf in range(m):
            core = 0 if w < full else 1 if w >= rpc - full else hf

            @pl.when((lon != me) | (core != lat))
            def _():
                remote(mixed.at[0, 0, 0], returned.at[r, hf], send2.at[0, 0, 0], recv2.at[r, hf], lon, core).wait_recv()
        att_t = returned[r].reshape(width, cells)
        update = dot(att_t, wout_ref[...], (0, 0))
        out_ref[r] = (fields_ref[r].astype(jnp.float32) + update).astype(jnp.bfloat16)

    each_forward(lambda copy: copy.wait_send())
    if shared is not None:
        for s in range(n):
            @pl.when((s != me) & (s % m == lat))
            def _():
                relay(s).wait_send()
    for slot in slots:
        for u in units(slot):
            for c in range(chips):
                row, hf, away, copy = back(slot, u, c)

                @pl.when(away)
                def _():
                    copy.wait_send()


def solution(mesh):
    n, m = mesh.shape["lon"], mesh.shape["lat"]

    def body(fields, norm_gain, w_qkv, w_out):
        rows, cells, width = fields.shape
        chips, rpc, full = plan(n, m, rows)
        groups, slots = n // chips, full + (1 if rpc % m else 0)
        queries, block = chips * cells, 2 * cells
        head_width = width // HEADS
        half = width // m
        bf16, f32 = jnp.bfloat16, jnp.float32
        return pl.pallas_call(
            functools.partial(kernel, n, m),
            out_shape=pltpu.VMEM(fields.shape, fields.dtype),
            in_specs=[pl.BlockSpec(memory_space=pltpu.HBM)] * 4,
            out_specs=pl.BlockSpec(memory_space=pltpu.VMEM),
            scratch_shapes=[
                pltpu.VMEM(fields.shape, fields.dtype),
                pltpu.VMEM((1, width), norm_gain.dtype),
                pltpu.VMEM(w_qkv.shape, w_qkv.dtype),
                pltpu.VMEM(w_out.shape, w_out.dtype),
                pltpu.VMEM((rows, cells, width), bf16),
                pltpu.VMEM((3 * width, width), bf16),
                pltpu.VMEM((slots, n, cells, width), bf16),
                pltpu.VMEM((block, queries), f32),
                pltpu.VMEM((block, queries), f32),
                pltpu.VMEM((slots, 2 * width, queries), bf16),
                pltpu.VMEM((block, 2 * width), bf16),
                pltpu.VMEM((width, block), bf16),
                pltpu.VMEM((slots * HEADS, 1, queries), f32),
                pltpu.VMEM((slots * HEADS, 8, queries), f32),
                pltpu.VMEM((slots * HEADS, head_width, queries), f32),
                pltpu.VMEM((slots, m, chips, half, cells), bf16),
                pltpu.VMEM((rows, m, half, cells), bf16),
                pltpu.SemaphoreType.DMA((4,)),
                pltpu.SemaphoreType.DMA((groups, rows)),
                pltpu.SemaphoreType.DMA((rows,)),
                pltpu.SemaphoreType.DMA((slots, n)),
                pltpu.SemaphoreType.DMA((n,)),
                pltpu.SemaphoreType.DMA((slots, m, chips)),
                pltpu.SemaphoreType.DMA((rows, m)),
            ],
            compiler_params=pltpu.CompilerParams(
                collective_id=0, has_side_effects=True, vmem_limit_bytes=40 * 2**20,
            ),
        )(*(
            pltpu.with_memory_space_constraint(x, pltpu.HBM)
            for x in (fields, norm_gain.reshape(1, width), w_qkv, w_out)
        ))

    return jax.shard_map(
        body,
        mesh=mesh,
        in_specs=(P(("groups", "lat"), "lon", None), P(), P(), P()),
        out_specs=P(("groups", "lat"), "lon", None),
        check_vma=False,
    )
```

time: 31.1 us -> 28.9 us (0.929)
  Pallas kernels: 30.3 us -> 27.8 us
    pallas_call x1, Pallas kernels: 30.3 us -> 27.8 us  [body(): pl.pallas_call(functools.partial(kernel, n, m), out_shape=pltpu.VMEM(fiel...]
where the time goes in v2:
time: 28.9 us; the launch traced here: 28.5 us
  Pallas kernels  27.8 us (96%)
  local copies, waits for them, and re-layouts  0.68 us (2%)
    pallas_call x1, Pallas kernels, body(): pl.pallas_call(functools.partial(kernel, n, m), out_shape=pltpu.VMEM(fiel...  27.8 us
    unnamed x1, local copies, waits for them, and re-layouts  0.68 us

profile of v2, /device:TPU:0, one launch (start us, length us, event | category | flops | bytes accessed | tf_op | source)
XLA Modules:
  0.0 28.5 jit_solution(7424962538789056798)
XLA Ops:
  0.0 27.8 %shard_map.46 = bf16[6,128,128]{2,1,0:T(8,128)(2,1)S(1)} custom-call(bf16[6,128,128]{2,1,0:T(8,128)(2,1)} %fields_hbm.1, f32[1,128]{1,0:T(1,128)} %bitcast.1, bf16[128,384]{1,0:T(8,128)(2,1)} %wqkv_hbm.1, bf16[128,128]{1,0:T(8,128)(2,1)} %wout_hbm.1), custom_call_target="tpu_custom_call" | custom-call | tf_op jit(solution)/shard_map/pallas_call | solution.py:322
  27.8 0.7 %copy.6 = bf16[6,128,128]{2,1,0:T(8,128)(2,1)} copy(bf16[6,128,128]{2,1,0:T(8,128)(2,1)S(1)} %shard_map.46) | data formatting | bytes 393216

commit v3 on v2

--- a/solution.py
+++ b/solution.py
@@ -25,8 +25,8 @@
 
 def kernel(n, m, fields_hbm, gain_hbm, wqkv_hbm, wout_hbm, out_ref,
            fields_ref, gain_ref, wqkv_ref, wout_ref,
-           normed, w_t, x, scores_a, scores_b, q_s, kk_s, v_s, top_s, sum_s, acc_s, mixed, returned,
-           loaded, send1, twin1, recv1, relayed, send2, recv2):
+           normed, w_t, twice_s, x, scores_s, p_s, q_s, kk_s, v_s, top_s, sum_s, acc_s, mixed, returned,
+           loaded, send1, twin1, recv1, relayed, send2, recv2, near, far):
     me, lat = lax.axis_index("lon"), lax.axis_index("lat")
     rows, cells, width = fields_ref.shape
     head_width = width // HEADS
@@ -38,6 +38,7 @@
     pair = 2
     block = pair * cells
     blocks = chips // pair
+    step = 32
     per_lat = chips // m
     group, chip = me // chips, lax.rem(me, chips)
     source_lat = chip // per_lat
@@ -48,12 +49,19 @@
     slots = list(range(full)) + ([full] if rpc % m else [])
 
     barrier = pltpu.get_barrier_semaphore()
-    for k in range(n):
-        for c in range(m):
-            if k or c:
-                pl.semaphore_signal(
-                    barrier, inc=1, device_id={"lon": lax.rem(me + k, n), "lat": lax.rem(lat + c, m)},
-                    device_id_type=MESH)
+
+    def greet(lon, core):
+        pl.semaphore_signal(barrier, inc=1, device_id={"lon": lon, "lat": core}, device_id_type=MESH)
+
+    for k in range(groups):
+        for c in range(chips):
+            lon = lax.rem(group + k, groups) * chips + c
+            if k:
+                greet(lon, m - 1)
+            else:
+                @pl.when((lon != me) | (lat != 0))
+                def _():
+                    greet(lon, 0)
 
     loads = [
         pltpu.make_async_copy(src, dst, loaded.at[i])
@@ -72,6 +80,17 @@
         center = jnp.mean(inputs, axis=-1, keepdims=True)
         spread = jnp.mean((inputs - center) ** 2, axis=-1, keepdims=True)
         normed[r] = ((inputs - center) * lax.rsqrt(spread + 1e-05) * gain).astype(jnp.bfloat16)
+
+    loads[2].wait()
+    loads[3].wait()
+    w_t[...] = wqkv_ref[...].astype(jnp.float32).T.astype(jnp.bfloat16)
+    for g in range(m):
+        w_k = w_t[width + g * half:width + (g + 1) * half, :]
+        twice_s[0, g] = jnp.concatenate([w_k, w_k], axis=0)
+    twice_s[1, 0] = twice_s[0, lat]
+    top_s[...] = jnp.full(top_s.shape, -jnp.inf, jnp.float32)
+    sum_s[...] = jnp.zeros(sum_s.shape, jnp.float32)
+    acc_s[...] = jnp.zeros(acc_s.shape, jnp.float32)
 
     def slot_row(slot):
         if slot == shared:
@@ -104,8 +123,8 @@
     order = [r for r in range(rows) if full <= r % rpc < rpc - full] + [
         r for r in range(rows) if not full <= r % rpc < rpc - full]
 
-    def each_forward(use):
-        for k in range(groups):
+    def each_forward(use, ks):
+        for k in ks:
             for r in order:
                 slot, away, copy, twin = forward(k, r)
                 if away is True:
@@ -121,20 +140,32 @@
                     def _():
                         use(twin)
 
-    pl.semaphore_wait(barrier, n * m - 1)
-    each_forward(lambda copy: copy.start())
+    @pl.when(lat == 0)
+    def _():
+        pl.semaphore_wait(barrier, chips * m - 1)
+        pl.semaphore_signal(near, inc=1, device_id={"lon": me, "lat": 1}, device_id_type=MESH)
+
+    @pl.when(lat != 0)
+    def _():
+        pl.semaphore_wait(near, 1)
+
+    each_forward(lambda copy: copy.start(), [0])
+
+    @pl.when(lat != 0)
+    def _():
+        pl.semaphore_wait(barrier, (n - chips) * m)
+        pl.semaphore_signal(far, inc=1, device_id={"lon": me, "lat": 0}, device_id_type=MESH)
+
+    @pl.when(lat == 0)
+    def _():
+        pl.semaphore_wait(far, 1)
+
+    each_forward(lambda copy: copy.start(), range(1, groups))
 
     @pl.when(mine)
     def _():
         for slot in slots:
             x[slot, me] = normed[slot_row(slot)]
-
-    loads[2].wait()
-    loads[3].wait()
-    w_t[...] = wqkv_ref[...].astype(jnp.float32).T.astype(jnp.bfloat16)
-    top_s[...] = jnp.full(top_s.shape, -jnp.inf, jnp.float32)
-    sum_s[...] = jnp.zeros(sum_s.shape, jnp.float32)
-    acc_s[...] = jnp.zeros(acc_s.shape, jnp.float32)
 
     def arrival(slot, s):
         return remote(normed.at[0], x.at[slot, s], send1.at[0, 0], recv1.at[slot, s], s, lat)
@@ -185,45 +216,56 @@
 
     def attend(slot, s0):
         heads = heads_of(slot)
-        span = heads * head_width
         cell_rows = x[slot, pl.ds(s0, pair)].reshape(block, width)
-        w_k = weight(1, slot)
-        if slot == shared:
-            kk_s[:, 0:2 * span] = dot(cell_rows, jnp.concatenate([w_k, w_k], axis=0), (1, 1)).astype(jnp.bfloat16)
-        else:
-            keys = dot(cell_rows, w_k, (1, 1)).astype(jnp.bfloat16)
-            kk_s[:, 0:span] = keys
-            kk_s[:, span:2 * span] = keys
-        v_s[0:span, :] = dot(weight(2, slot), cell_rows, (1, 1)).astype(jnp.bfloat16)
+        for g in range(heads // share):
+            kk_s[g] = dot(cell_rows, twice_s[int(slot == shared), g], (1, 1)).astype(jnp.bfloat16)
+        v_s[0:heads * head_width, :] = dot(weight(2, slot), cell_rows, (1, 1)).astype(jnp.bfloat16)
 
         def gap(size):
             return [jnp.zeros((size, queries), jnp.bfloat16)] if size else []
 
-        def first_pass(h):
+        def scores(h):
+            g, at = h // share, h % share * head_width
             lo, hi = h * head_width, (h + 1) * head_width
+            before, after = gap(at), gap(half - head_width - at)
             spread_q = jnp.concatenate(
-                gap(lo) + [q_s[slot, lo:hi, :]] + gap(span - hi + lo) + [q_s[slot, width + lo:width + hi, :]]
-                + gap(span - hi), axis=0)
-            s = dot(kk_s[:, 0:2 * span], spread_q, (1, 0))
-            (scores_a, scores_b)[h % 2][...] = s
-            return jnp.max(jnp.max(s.reshape(block // 8, 8, queries), axis=0), axis=0, keepdims=True)
-
-        def second_pass(h, highest):
+                before + [q_s[slot, lo:hi, :]] + after + before + [q_s[slot, width + lo:width + hi, :]] + after, axis=0)
+            return dot(kk_s[g], spread_q, (1, 0))
+
+        def keep(h, s, c, part):
+            piece = s[c * step:(c + 1) * step]
+            scores_s[h % 2, c * step:(c + 1) * step, :] = piece
+            part_max = jnp.max(piece.reshape(step // 8, 8, queries), axis=0)
+            return part_max if part is None else jnp.maximum(part, part_max)
+
+        def weigh(h, fade):
+            at = slot * HEADS + h
+            acc_s[at] = acc_s[at] * fade + dot(v_s[h * head_width:(h + 1) * head_width, :], p_s[h % 2], (1, 0))
+
+        s, part = scores(0), None
+        for c in range(block // step):
+            part = keep(0, s, c, part)
+        fades = {}
+        for h in range(heads):
+            highest = jnp.max(part, axis=0, keepdims=True)
+            s = scores(h + 1) if h + 1 < heads else None
+            if h:
+                weigh(h - 1, fades[h - 1])
             at = slot * HEADS + h
             before = top_s[at]
             now = jnp.maximum(before, highest)
-            fade = jnp.exp2(before - now)
+            fades[h] = jnp.exp2(before - now)
             top_s[at] = now
-            p = jnp.exp2((scores_a, scores_b)[h % 2][...] - now)
-            sum_s[at] = sum_s[at] * fade + jnp.sum(p.reshape(block // 8, 8, queries), axis=0)
-            acc_s[at] = acc_s[at] * fade + dot(
-                v_s[h * head_width:(h + 1) * head_width, :], p.astype(jnp.bfloat16), (1, 0))
-
-        highest = first_pass(0)
-        for h in range(heads):
-            following = first_pass(h + 1) if h + 1 < heads else None
-            second_pass(h, highest)
-            highest = following
+            part = total = None
+            for c in range(block // step):
+                p = jnp.exp2(scores_s[h % 2, c * step:(c + 1) * step, :] - now)
+                piece = jnp.sum(p.reshape(step // 8, 8, queries), axis=0)
+                total = piece if total is None else total + piece
+                p_s[h % 2, c * step:(c + 1) * step, :] = p.astype(jnp.bfloat16)
+                if s is not None:
+                    part = keep(h + 1, s, c, part)
+            sum_s[at] = sum_s[at] * fades[h] + total
+        weigh(heads - 1, fades[heads - 1])
 
     def attend_group(slot, k):
         theirs = lax.rem(group + k, groups)
@@ -292,7 +334,7 @@
         update = dot(att_t, wout_ref[...], (0, 0))
         out_ref[r] = (fields_ref[r].astype(jnp.float32) + update).astype(jnp.bfloat16)
 
-    each_forward(lambda copy: copy.wait_send())
+    each_forward(lambda copy: copy.wait_send(), range(groups))
     if shared is not None:
         for s in range(n):
             @pl.when((s != me) & (s % m == lat))
@@ -331,11 +373,12 @@
                 pltpu.VMEM(w_out.shape, w_out.dtype),
                 pltpu.VMEM((rows, cells, width), bf16),
                 pltpu.VMEM((3 * width, width), bf16),
+                pltpu.VMEM((2, m, 2 * half, width), bf16),
                 pltpu.VMEM((slots, n, cells, width), bf16),
-                pltpu.VMEM((block, queries), f32),
-                pltpu.VMEM((block, queries), f32),
+                pltpu.VMEM((2, block, queries), f32),
+                pltpu.VMEM((2, block, queries), bf16),
                 pltpu.VMEM((slots, 2 * width, queries), bf16),
-                pltpu.VMEM((block, 2 * width), bf16),
+                pltpu.VMEM((m, block, 2 * half), bf16),
                 pltpu.VMEM((width, block), bf16),
                 pltpu.VMEM((slots * HEADS, 1, queries), f32),
                 pltpu.VMEM((slots * HEADS, 8, queries), f32),
@@ -349,6 +392,8 @@
                 pltpu.SemaphoreType.DMA((n,)),
                 pltpu.SemaphoreType.DMA((slots, m, chips)),
                 pltpu.SemaphoreType.DMA((rows, m)),
+                pltpu.SemaphoreType.REGULAR,
+                pltpu.SemaphoreType.REGULAR,
             ],
             compiler_params=pltpu.CompilerParams(
                 collective_id=0, has_side_effects=True, vmem_limit_bytes=40 * 2**20,

time: 28.9 us -> 26.4 us (0.913)
  the two profiles are of different devices: /device:TPU:0 before, /device:TPU:17 now
where the time goes in v3:
time: 26.4 us; the launch traced here: 26.3 us
  Pallas kernels  25.6 us (97%)
  local copies, waits for them, and re-layouts  0.68 us (3%)
    pallas_call x1, Pallas kernels, body(): pl.pallas_call(functools.partial(kernel, n, m), out_shape=pltpu.VMEM(fiel...  25.6 us
    unnamed x1, local copies, waits for them, and re-layouts  0.68 us

profile of v3, /device:TPU:17, one launch (start us, length us, event | category | flops | bytes accessed | tf_op | source)
XLA Modules:
  0.0 26.3 jit_solution(7369634169870717887)
XLA Ops:
  0.0 25.6 %shard_map.46 = bf16[6,128,128]{2,1,0:T(8,128)(2,1)S(1)} custom-call(bf16[6,128,128]{2,1,0:T(8,128)(2,1)} %fields_hbm.1, f32[1,128]{1,0:T(1,128)} %bitcast.1, bf16[128,384]{1,0:T(8,128)(2,1)} %wqkv_hbm.1, bf16[128,128]{1,0:T(8,128)(2,1)} %wout_hbm.1), custom_call_target="tpu_custom_call" | custom-call | tf_op jit(solution)/shard_map/pallas_call | solution.py:364
  25.6 0.7 %copy.6 = bf16[6,128,128]{2,1,0:T(8,128)(2,1)} copy(bf16[6,128,128]{2,1,0:T(8,128)(2,1)S(1)} %shard_map.46) | data formatting | bytes 393216

commit v4 on v3

--- a/solution.py
+++ b/solution.py
@@ -9,6 +9,7 @@
 from jax.sharding import PartitionSpec as P
 
 HEADS = 8
+TILE = 256
 LOG2E = math.log2(math.e)
 MESH = pl.DeviceIdType.MESH
 
@@ -214,79 +215,77 @@
             q_s[slot, 0:span, b * block:(b + 1) * block] = q_hi
             q_s[slot, width:width + span, b * block:(b + 1) * block] = q_lo
 
-    def attend(slot, s0):
-        heads = heads_of(slot)
+    def units(slot):
+        return [0] if slot == shared else list(range(m))
+
+    def prepare(slot, b, s0):
         cell_rows = x[slot, pl.ds(s0, pair)].reshape(block, width)
-        for g in range(heads // share):
-            kk_s[g] = dot(cell_rows, twice_s[int(slot == shared), g], (1, 1)).astype(jnp.bfloat16)
-        v_s[0:heads * head_width, :] = dot(weight(2, slot), cell_rows, (1, 1)).astype(jnp.bfloat16)
-
-        def gap(size):
-            return [jnp.zeros((size, queries), jnp.bfloat16)] if size else []
-
-        def scores(h):
-            g, at = h // share, h % share * head_width
+        for u in units(slot):
+            kk_s[slot, u, b * block:(b + 1) * block, :] = dot(
+                cell_rows, twice_s[int(slot == shared), u], (1, 1)).astype(jnp.bfloat16)
+        v_s[slot, 0:heads_of(slot) * head_width, b * block:(b + 1) * block] = dot(
+            weight(2, slot), cell_rows, (1, 1)).astype(jnp.bfloat16)
+
+    def gap(size):
+        return [jnp.zeros((size, queries), jnp.bfloat16)] if size else []
+
+    def attend(items):
+        def scores(slot, h, first, size):
+            u, at = h // share, h % share * head_width
             lo, hi = h * head_width, (h + 1) * head_width
             before, after = gap(at), gap(half - head_width - at)
             spread_q = jnp.concatenate(
                 before + [q_s[slot, lo:hi, :]] + after + before + [q_s[slot, width + lo:width + hi, :]] + after, axis=0)
-            return dot(kk_s[g], spread_q, (1, 0))
-
-        def keep(h, s, c, part):
+            return dot(kk_s[slot, u, first:first + size, :], spread_q, (1, 0))
+
+        def keep(i, s, c, part):
             piece = s[c * step:(c + 1) * step]
-            scores_s[h % 2, c * step:(c + 1) * step, :] = piece
+            scores_s[i % 2, c * step:(c + 1) * step, :] = piece
             part_max = jnp.max(piece.reshape(step // 8, 8, queries), axis=0)
             return part_max if part is None else jnp.maximum(part, part_max)
 
-        def weigh(h, fade):
+        def weigh(i, fade):
+            slot, h, first, size = items[i]
             at = slot * HEADS + h
-            acc_s[at] = acc_s[at] * fade + dot(v_s[h * head_width:(h + 1) * head_width, :], p_s[h % 2], (1, 0))
-
-        s, part = scores(0), None
-        for c in range(block // step):
+            acc_s[at] = acc_s[at] * fade + dot(
+                v_s[slot, h * head_width:(h + 1) * head_width, first:first + size], p_s[i % 2, 0:size], (1, 0))
+
+        s, part = scores(*items[0]), None
+        for c in range(items[0][3] // step):
             part = keep(0, s, c, part)
-        fades = {}
-        for h in range(heads):
+        fade = None
+        for i, (slot, h, first, size) in enumerate(items):
             highest = jnp.max(part, axis=0, keepdims=True)
-            s = scores(h + 1) if h + 1 < heads else None
-            if h:
-                weigh(h - 1, fades[h - 1])
+            s = scores(*items[i + 1]) if i + 1 < len(items) else None
+            if i:
+                weigh(i - 1, fade)
             at = slot * HEADS + h
             before = top_s[at]
             now = jnp.maximum(before, highest)
-            fades[h] = jnp.exp2(before - now)
+            fade = jnp.exp2(before - now)
             top_s[at] = now
             part = total = None
-            for c in range(block // step):
-                p = jnp.exp2(scores_s[h % 2, c * step:(c + 1) * step, :] - now)
+            for c in range(size // step):
+                p = jnp.exp2(scores_s[i % 2, c * step:(c + 1) * step, :] - now)
                 piece = jnp.sum(p.reshape(step // 8, 8, queries), axis=0)
                 total = piece if total is None else total + piece
-                p_s[h % 2, c * step:(c + 1) * step, :] = p.astype(jnp.bfloat16)
+                p_s[i % 2, c * step:(c + 1) * step, :] = p.astype(jnp.bfloat16)
                 if s is not None:
-                    part = keep(h + 1, s, c, part)
-            sum_s[at] = sum_s[at] * fades[h] + total
-        weigh(heads - 1, fades[heads - 1])
-
-    def attend_group(slot, k):
-        theirs = lax.rem(group + k, groups)
-
-        def one_block(b, carry):
-            at = jnp.where(theirs > group, b, blocks - 1 - b) if k else b
-            s0 = theirs * chips + at * pair
-            if k:
-                for i in range(pair):
-                    await_source(slot, s0 + i)
-            attend(slot, s0)
-            return carry
-
-        if not k:
-            for c in range(chips):
-                await_source(slot, theirs * chips + c)
-            project_queries(slot)
-        lax.fori_loop(0, blocks, one_block, 0)
-
-    def units(slot):
-        return [0] if slot == shared else list(range(m))
+                    part = keep(i + 1, s, c, part)
+            sum_s[at] = sum_s[at] * fade + total
+        weigh(len(items) - 1, fade)
+
+    def await_group(slot, k):
+        for c in range(chips):
+            await_source(slot, lax.rem(group + k, groups) * chips + c)
+
+    def prepare_group(slot, k):
+        for b in range(blocks):
+            prepare(slot, b, lax.rem(group + k, groups) * chips + b * pair)
+
+    def unit_items(slot, u):
+        wide = min(TILE, queries)
+        return [(slot, u * share + h, first, wide) for first in range(0, queries, wide) for h in range(share)]
 
     def back(slot, u, c):
         hf = lat if slot == shared else u
@@ -296,30 +295,38 @@
                       lon, source_lat)
         return row, hf, (lon != me) | (source_lat != lat), copy
 
-    def hand_back(slot):
-        for u in units(slot):
-            for j in range(share):
-                at = slot * HEADS + u * share + j
-                done = (acc_s[at] / jnp.sum(sum_s[at], axis=0, keepdims=True)).astype(jnp.bfloat16)
-                for c in range(chips):
-                    mixed[slot, u, c, j * head_width:(j + 1) * head_width, :] = done[:, c * cells:(c + 1) * cells]
+    def hand_back(slot, u):
+        for j in range(share):
+            at = slot * HEADS + u * share + j
+            done = (acc_s[at] / jnp.sum(sum_s[at], axis=0, keepdims=True)).astype(jnp.bfloat16)
             for c in range(chips):
-                row, hf, away, copy = back(slot, u, c)
-
-                @pl.when(away)
-                def _():
-                    copy.start()
-
-                @pl.when(jnp.logical_not(away))
-                def _():
-                    returned[row, hf] = mixed[slot, u, c]
-
-    for k in range(groups):
+                mixed[slot, u, c, j * head_width:(j + 1) * head_width, :] = done[:, c * cells:(c + 1) * cells]
+        for c in range(chips):
+            row, hf, away, copy = back(slot, u, c)
+
+            @pl.when(away)
+            def _():
+                copy.start()
+
+            @pl.when(jnp.logical_not(away))
+            def _():
+                returned[row, hf] = mixed[slot, u, c]
+
+    pass_on(0)
+    for slot in slots:
+        await_group(slot, 0)
+        project_queries(slot)
+        prepare_group(slot, 0)
+        attend([item for u in units(slot) for item in unit_items(slot, u)])
+    for k in range(1, groups):
         pass_on(k)
-        for slot in (slots if not k else slots[::-1]):
-            attend_group(slot, k)
-            if k == groups - 1:
-                hand_back(slot)
+        for slot in slots[::-1]:
+            await_group(slot, k)
+            prepare_group(slot, k)
+            for u in units(slot):
+                attend(unit_items(slot, u))
+                if k == groups - 1:
+                    hand_back(slot, u)
 
     for r in range(rows):
         w = r % rpc
@@ -375,11 +382,11 @@
                 pltpu.VMEM((3 * width, width), bf16),
                 pltpu.VMEM((2, m, 2 * half, width), bf16),
                 pltpu.VMEM((slots, n, cells, width), bf16),
-                pltpu.VMEM((2, block, queries), f32),
-                pltpu.VMEM((2, block, queries), bf16),
+                pltpu.VMEM((2, min(TILE, queries), queries), f32),
+                pltpu.VMEM((2, min(TILE, queries), queries), bf16),
                 pltpu.VMEM((slots, 2 * width, queries), bf16),
-                pltpu.VMEM((m, block, 2 * half), bf16),
-                pltpu.VMEM((width, block), bf16),
+                pltpu.VMEM((slots, m, queries, 2 * half), bf16),
+                pltpu.VMEM((slots, width, queries), bf16),
                 pltpu.VMEM((slots * HEADS, 1, queries), f32),
                 pltpu.VMEM((slots * HEADS, 8, queries), f32),
                 pltpu.VMEM((slots * HEADS, head_width, queries), f32),

time: 26.4 us -> 24.2 us (0.917)
  the two profiles are of different devices: /device:TPU:17 before, /device:TPU:0 now
where the time goes in v4:
time: 24.2 us; the launch traced here: 23.8 us
  Pallas kernels  23.1 us (95%)
  local copies, waits for them, and re-layouts  0.68 us (3%)
    pallas_call x1, Pallas kernels, body(): pl.pallas_call(functools.partial(kernel, n, m), out_shape=pltpu.VMEM(fiel...  23.1 us
    unnamed x1, local copies, waits for them, and re-layouts  0.68 us

profile of v4, /device:TPU:0, one launch (start us, length us, event | category | flops | bytes accessed | tf_op | source)
XLA Modules:
  0.0 23.8 jit_solution(4801600928820236267)
XLA Ops:
  0.0 23.1 %shard_map.46 = bf16[6,128,128]{2,1,0:T(8,128)(2,1)S(1)} custom-call(bf16[6,128,128]{2,1,0:T(8,128)(2,1)} %fields_hbm.1, f32[1,128]{1,0:T(1,128)} %bitcast.1, bf16[128,384]{1,0:T(8,128)(2,1)} %wqkv_hbm.1, bf16[128,128]{1,0:T(8,128)(2,1)} %wout_hbm.1), custom_call_target="tpu_custom_call" | custom-call | tf_op jit(solution)/shard_map/pallas_call | solution.py:371
  23.1 0.7 %copy.6 = bf16[6,128,128]{2,1,0:T(8,128)(2,1)} copy(bf16[6,128,128]{2,1,0:T(8,128)(2,1)S(1)} %shard_map.46) | data formatting | bytes 393216

commit v5 on v4

--- a/solution.py
+++ b/solution.py
@@ -27,7 +27,7 @@
 def kernel(n, m, fields_hbm, gain_hbm, wqkv_hbm, wout_hbm, out_ref,
            fields_ref, gain_ref, wqkv_ref, wout_ref,
            normed, w_t, twice_s, x, scores_s, p_s, q_s, kk_s, v_s, top_s, sum_s, acc_s, mixed, returned,
-           loaded, send1, twin1, recv1, relayed, send2, recv2, near, far):
+           loaded, send1, twin1, recv1, relayed, send2, recv2, near, far, deep):
     me, lat = lax.axis_index("lon"), lax.axis_index("lat")
     rows, cells, width = fields_ref.shape
     head_width = width // HEADS
@@ -54,10 +54,17 @@
     def greet(lon, core):
         pl.semaphore_signal(barrier, inc=1, device_id={"lon": lon, "lat": core}, device_id_type=MESH)
 
+    relayed_word = groups == 2 and m == 2 and per_lat == pair
+    at_border = chip // pair == 1 - group
+    outward = pair * (2 * group - 1)
     for k in range(groups):
         for c in range(chips):
             lon = lax.rem(group + k, groups) * chips + c
-            if k:
+            if k and relayed_word:
+                @pl.when(at_border)
+                def _():
+                    greet(lon, m - 1)
+            elif k:
                 greet(lon, m - 1)
             else:
                 @pl.when((lon != me) | (lat != 0))
@@ -81,17 +88,6 @@
         center = jnp.mean(inputs, axis=-1, keepdims=True)
         spread = jnp.mean((inputs - center) ** 2, axis=-1, keepdims=True)
         normed[r] = ((inputs - center) * lax.rsqrt(spread + 1e-05) * gain).astype(jnp.bfloat16)
-
-    loads[2].wait()
-    loads[3].wait()
-    w_t[...] = wqkv_ref[...].astype(jnp.float32).T.astype(jnp.bfloat16)
-    for g in range(m):
-        w_k = w_t[width + g * half:width + (g + 1) * half, :]
-        twice_s[0, g] = jnp.concatenate([w_k, w_k], axis=0)
-    twice_s[1, 0] = twice_s[0, lat]
-    top_s[...] = jnp.full(top_s.shape, -jnp.inf, jnp.float32)
-    sum_s[...] = jnp.zeros(sum_s.shape, jnp.float32)
-    acc_s[...] = jnp.zeros(acc_s.shape, jnp.float32)
 
     def slot_row(slot):
         if slot == shared:
@@ -124,9 +120,11 @@
     order = [r for r in range(rows) if full <= r % rpc < rpc - full] + [
         r for r in range(rows) if not full <= r % rpc < rpc - full]
 
+    cross_order = sorted(order, key=lambda r: (order.index(r) >= rows // rpc, r % rpc, -r))
+
     def each_forward(use, ks):
         for k in ks:
-            for r in order:
+            for r in (cross_order if k else order):
                 slot, away, copy, twin = forward(k, r)
                 if away is True:
                     use(copy)
@@ -154,14 +152,39 @@
 
     @pl.when(lat != 0)
     def _():
-        pl.semaphore_wait(barrier, (n - chips) * m)
+        pl.semaphore_wait(barrier, pair * m if relayed_word else (n - chips) * m)
         pl.semaphore_signal(far, inc=1, device_id={"lon": me, "lat": 0}, device_id_type=MESH)
+        if relayed_word:
+            @pl.when(at_border)
+            def _():
+                pl.semaphore_signal(
+                    deep, inc=1, device_id={"lon": (1 - group) * chips + chip + outward, "lat": group}, device_id_type=MESH)
 
     @pl.when(lat == 0)
     def _():
         pl.semaphore_wait(far, 1)
 
+    if relayed_word:
+        @pl.when(lat != group)
+        def _():
+            pl.semaphore_wait(deep, 1)
+
+            @pl.when(at_border)
+            def _():
+                pl.semaphore_signal(deep, inc=1, device_id={"lon": me + outward, "lat": lat}, device_id_type=MESH)
+
     each_forward(lambda copy: copy.start(), range(1, groups))
+
+    loads[2].wait()
+    loads[3].wait()
+    w_t[...] = wqkv_ref[...].astype(jnp.float32).T.astype(jnp.bfloat16)
+    for g in range(m):
+        w_k = w_t[width + g * half:width + (g + 1) * half, :]
+        twice_s[0, g] = jnp.concatenate([w_k, w_k], axis=0)
+    twice_s[1, 0] = twice_s[0, lat]
+    top_s[...] = jnp.full(top_s.shape, -jnp.inf, jnp.float32)
+    sum_s[...] = jnp.zeros(sum_s.shape, jnp.float32)
+    acc_s[...] = jnp.zeros(acc_s.shape, jnp.float32)
 
     @pl.when(mine)
     def _():
@@ -328,6 +351,21 @@
                 if k == groups - 1:
                     hand_back(slot, u)
 
+    each_forward(lambda copy: copy.wait_send(), range(groups))
+    if shared is not None:
+        for s in range(n):
+            @pl.when((s != me) & (s % m == lat))
+            def _():
+                relay(s).wait_send()
+    for slot in slots:
+        for u in units(slot):
+            for c in range(chips):
+                row, hf, away, copy = back(slot, u, c)
+
+                @pl.when(away)
+                def _():
+                    copy.wait_send()
+
     for r in range(rows):
         w = r % rpc
         lon = group * chips + lat * per_lat + r // rpc
@@ -340,21 +378,6 @@
         att_t = returned[r].reshape(width, cells)
         update = dot(att_t, wout_ref[...], (0, 0))
         out_ref[r] = (fields_ref[r].astype(jnp.float32) + update).astype(jnp.bfloat16)
-
-    each_forward(lambda copy: copy.wait_send(), range(groups))
-    if shared is not None:
-        for s in range(n):
-            @pl.when((s != me) & (s % m == lat))
-            def _():
-                relay(s).wait_send()
-    for slot in slots:
-        for u in units(slot):
-            for c in range(chips):
-                row, hf, away, copy = back(slot, u, c)
-
-                @pl.when(away)
-                def _():
-                    copy.wait_send()
 
 
 def solution(mesh):
@@ -401,6 +424,7 @@
                 pltpu.SemaphoreType.DMA((rows, m)),
                 pltpu.SemaphoreType.REGULAR,
                 pltpu.SemaphoreType.REGULAR,
+                pltpu.SemaphoreType.REGULAR,
             ],
             compiler_params=pltpu.CompilerParams(
                 collective_id=0, has_side_effects=True, vmem_limit_bytes=40 * 2**20,

time: 24.2 us -> 23.3 us (0.963)
  the two profiles are of different devices: /device:TPU:0 before, /device:TPU:1 now
where the time goes in v5:
time: 23.3 us; the launch traced here: 23.1 us
  Pallas kernels  22.4 us (96%)
  local copies, waits for them, and re-layouts  0.68 us (3%)
    pallas_call x1, Pallas kernels, body(): pl.pallas_call(functools.partial(kernel, n, m), out_shape=pltpu.VMEM(fiel...  22.4 us
    unnamed x1, local copies, waits for them, and re-layouts  0.68 us

profile of v5, /device:TPU:1, one launch (start us, length us, event | category | flops | bytes accessed | tf_op | source)
XLA Modules:
  0.0 23.1 jit_solution(7059985175564165790)
XLA Ops:
  0.0 22.4 %shard_map.46 = bf16[6,128,128]{2,1,0:T(8,128)(2,1)S(1)} custom-call(bf16[6,128,128]{2,1,0:T(8,128)(2,1)} %fields_hbm.1, f32[1,128]{1,0:T(1,128)} %bitcast.1, bf16[128,384]{1,0:T(8,128)(2,1)} %wqkv_hbm.1, bf16[128,128]{1,0:T(8,128)(2,1)} %wout_hbm.1), custom_call_target="tpu_custom_call" | custom-call | tf_op jit(solution)/shard_map/pallas_call | solution.py:394
  22.5 0.7 %copy.6 = bf16[6,128,128]{2,1,0:T(8,128)(2,1)} copy(bf16[6,128,128]{2,1,0:T(8,128)(2,1)S(1)} %shard_map.46) | data formatting | bytes 393216
